TPU v7x, 8 devices: a whole 2x2x1 slice. The times are simulated.
8 devices in a mesh: data: 1 (over z), stage: 8 (over y, x, core).
Axes of the slice: x: 2, y: 2, z: 1, core: 2. Of those that a mesh axis runs over, the one named last changes fastest.
Arguments:
- x_init: float32 [32, 64, 64], P('data')
- h_warm: bfloat16 [7, 32, 64, 384], P(None, 'data')
- w_lat: bfloat16 [8, 64, 384], P('stage')
- w_qkv: bfloat16 [8, 384, 1152], P('stage')
- w_o: bfloat16 [8, 6, 64, 384], P('stage')
- w_up: bfloat16 [8, 384, 1536], P('stage')
- w_down: bfloat16 [8, 1536, 384], P('stage')
- w_out: bfloat16 [384, 64], replicated
- ada_mods: float32 [4, 8, 6, 384], P(None, 'stage')
- alpha_coef: float32 [4], replicated
- beta_coef: float32 [4], replicated
Outputs:
- output 1: float32 [32, 64, 64], P('data')
- output 2: bfloat16 [8, 32, 64, 384], P('stage', 'data')
All inputs are finite; a program needn't handle non-finite values.
Results may differ from a plain program's by a relative error of at most 0.02.
Values are sent between devices in bfloat16 or wider.
A program may use at most 1 GiB of HBM per device.

v0:
```python
import functools
import math

import jax
import jax.numpy as jnp
from jax import lax
from jax.experimental import pallas as pl
from jax.experimental.pallas import tpu as pltpu
from jax.sharding import PartitionSpec as P

MESH = pl.DeviceIdType.MESH
F32, BF16 = jnp.float32, jnp.bfloat16
MICRO = 4
GROUP = 256
TILE = 128
GELU_A = math.sqrt(2.0 / math.pi)
GELU_B = 0.044715


def dot(lhs, rhs):
    return lax.dot_general(lhs, rhs, (((1,), (0,)), ((), ())), preferred_element_type=F32)


def layer_norm(h, scale, shift):
    mean = jnp.sum(h, axis=0, keepdims=True) * (1.0 / h.shape[0])
    centered = h - mean
    var = jnp.sum(centered * centered, axis=0, keepdims=True) * (1.0 / h.shape[0])
    return centered * lax.rsqrt(var + 1e-6) * scale + shift


def kernel(dims, x_hbm, warm_hbm, wlat_hbm, wqkv_hbm, wo_hbm, wup_hbm, wdown_hbm, wout_hbm, mods_ref, alpha_ref, beta_ref,
           xo_ref, hl_ref,
           wlat_raw, wqkv_raw, wo_raw, wup_raw, wdown_raw, wout_raw, warm_raw, x_raw,
           wlat_t, wqkv_t, wo_t, wup_t, wdown_t, wout_t, modb,
           h_ref, u_ref, qkv_ref, att_ref, hid_ref, out_ref,
           b_in, x_in, b_out, x_f32, x_fin,
           load_sem, hs_sem, hr_sem, xs_sem, xr_sem, fs_sem, fr_sem):
    steps, stages, heads, head_dim, dim, micro, tm = dims
    stage = lax.axis_index('stage')
    last = stages - 1
    hidden = wup_t.shape[0]

    loads = [pltpu.make_async_copy(src, dst, load_sem.at[i]) for i, (src, dst) in enumerate((
        (x_hbm, x_raw), (wlat_hbm, wlat_raw), (wqkv_hbm, wqkv_raw), (wo_hbm, wo_raw),
        (wup_hbm, wup_raw), (wdown_hbm, wdown_raw), (wout_hbm, wout_raw)))]
    warm = pltpu.make_async_copy(warm_hbm.at[jnp.maximum(stage - 1, 0)], warm_raw, load_sem.at[7])
    for copy in loads:
        copy.start()
    warm.start()

    barrier = pltpu.get_barrier_semaphore()
    for shift in range(1, stages):
        pl.semaphore_signal(barrier, inc=1, device_id={'stage': lax.rem(stage + shift, stages)}, device_id_type=MESH)

    def mods_body(t, carry):
        for i in range(6):
            row = mods_ref[t, i:i + 1, :]
            if i in (1, 4):
                row = row + 1.0
            modb[t, i] = jnp.broadcast_to(row, (TILE, dim)).T
        return carry
    lax.fori_loop(0, steps, mods_body, 0)

    for copy in loads:
        copy.wait()
    warm.wait()
    wlat_t[...] = wlat_raw[...].T
    wqkv_t[...] = wqkv_raw[...].T
    wo_t[...] = wo_raw[...].T
    for j in range(hidden // dim):
        wup_t[j * dim:(j + 1) * dim, :] = wup_raw[:, j * dim:(j + 1) * dim].T * jnp.asarray(0.5, BF16)
        wdown_t[:, j * dim:(j + 1) * dim] = wdown_raw[j * dim:(j + 1) * dim, :].T
    wout_t[...] = wout_raw[...].T

    def init_body(m, carry):
        xt = x_raw[pl.ds(m * tm, tm), :].T
        x_f32[m] = xt
        x_in[0, m] = xt.astype(BF16)

        @pl.when(stage > 0)
        def _():
            b_in[0, m] = warm_raw[pl.ds(m * tm, tm), :].T

        @pl.when(stage == 0)
        def _():
            for t in range(steps):
                b_in[t, m] = jnp.zeros((dim, tm), BF16)
        return carry
    lax.fori_loop(0, micro, init_body, 0)

    pl.semaphore_wait(barrier, stages - 1)

    def h_copy(t, m):
        return pltpu.make_async_remote_copy(
            src_ref=b_out.at[t, m], dst_ref=b_in.at[t + 1, m], send_sem=hs_sem.at[t, m], recv_sem=hr_sem.at[t, m],
            device_id={'stage': jnp.minimum(stage + 1, last)}, device_id_type=MESH)

    def x_copy(t, m, dev):
        return pltpu.make_async_remote_copy(
            src_ref=x_in.at[t + 1, m], dst_ref=x_in.at[t + 1, m], send_sem=xs_sem.at[t, m, dev], recv_sem=xr_sem.at[t, m],
            device_id={'stage': dev}, device_id_type=MESH)

    def f_copy(m, dev):
        return pltpu.make_async_remote_copy(
            src_ref=x_fin.at[m], dst_ref=x_fin.at[m], send_sem=fs_sem.at[m, dev], recv_sem=fr_sem.at[m],
            device_id={'stage': dev}, device_id_type=MESH)

    low_half = lax.rem(lax.broadcasted_iota(jnp.int32, (head_dim, 2 * TILE), 1), TILE) < head_dim
    score_scale = head_dim ** -0.5 * math.log2(math.e)

    def attention(cols):
        zero_q = jnp.zeros((head_dim, TILE), BF16)
        zero_p = jnp.zeros((TILE, TILE), BF16)
        for hp in range(heads // 2):
            rows = slice(hp * TILE, (hp + 1) * TILE)
            q_pair = qkv_ref[hp * TILE:(hp + 1) * TILE, cols]
            k_pair = qkv_ref[dim + hp * TILE:dim + (hp + 1) * TILE, cols].T
            v_pair = qkv_ref[2 * dim + hp * TILE:2 * dim + (hp + 1) * TILE, cols]
            probs = []
            for sp in range(GROUP // TILE):
                span = slice(sp * TILE, (sp + 1) * TILE)
                q_blk = jnp.concatenate([
                    jnp.concatenate([q_pair[:head_dim, span], zero_q], axis=1),
                    jnp.concatenate([zero_q, q_pair[head_dim:, span]], axis=1)], axis=0)
                scores = dot(k_pair[span, :], q_blk)
                scores = jnp.where(low_half, scores[:head_dim], scores[head_dim:])
                top = jnp.max(scores, axis=0, keepdims=True)
                expd = jnp.exp2((scores - top) * score_scale)
                prob = expd * (1.0 / jnp.sum(expd, axis=0, keepdims=True))
                probs.append(jnp.concatenate([
                    jnp.where(low_half, prob, 0.0).astype(BF16), jnp.where(low_half, 0.0, prob).astype(BF16)], axis=0))
            for j in range(2):
                span = slice(j * TILE, (j + 1) * TILE)
                p_blk = jnp.concatenate([
                    jnp.concatenate([probs[0][:, span], zero_p], axis=1),
                    jnp.concatenate([zero_p, probs[1][:, span]], axis=1)], axis=0)
                out = dot(v_pair[j * head_dim:(j + 1) * head_dim, :], p_blk)
                att_ref[hp * TILE + j * head_dim:hp * TILE + (j + 1) * head_dim, cols] = out.astype(BF16)

    tiles = [slice(i * TILE, (i + 1) * TILE) for i in range(tm // TILE)]

    def slot_body(slot, carry):
        t, m = lax.div(slot, micro), lax.rem(slot, micro)

        @pl.when(jnp.logical_and(t > 0, stage > 0))
        def _():
            h_copy(t - 1, m).wait_recv()

        @pl.when(jnp.logical_and(t > 0, stage < last))
        def _():
            x_copy(t - 1, m, 0).wait_recv()

        h_ref[...] = b_in[t, m].astype(F32) + dot(wlat_t[...], x_in[t, m])
        for tile in tiles:
            u_ref[:, tile] = layer_norm(h_ref[:, tile], modb[t, 1], modb[t, 0]).astype(BF16)
        for j in range(3):
            rows = slice(j * dim, (j + 1) * dim)
            qkv_ref[rows, :] = dot(wqkv_t[rows, :], u_ref[...]).astype(BF16)
        for g in range(tm // GROUP):
            attention(slice(g * GROUP, (g + 1) * GROUP))
        proj = dot(wo_t[...], att_ref[...])
        for tile in tiles:
            h_new = h_ref[:, tile] + modb[t, 2] * proj[:, tile]
            h_ref[:, tile] = h_new
            u_ref[:, tile] = layer_norm(h_new, modb[t, 4], modb[t, 3]).astype(BF16)
        for j in range(hidden // GROUP):
            rows = slice(j * GROUP, (j + 1) * GROUP)
            half = dot(wup_t[rows, :], u_ref[...])
            inner = half * (half * half * (8.0 * GELU_A * GELU_B) + 2.0 * GELU_A)
            hid_ref[rows, :] = (half + half * jnp.tanh(inner)).astype(BF16)
        down = dot(wdown_t[...], hid_ref[...])
        for tile in tiles:
            out_ref[:, tile] = (h_ref[:, tile] + modb[t, 5] * down[:, tile]).astype(BF16)

        @pl.when(jnp.logical_and(t < steps - 1, stage < last))
        def _():
            b_out[t, m] = out_ref[...]
            h_copy(t, m).start()

        @pl.when(t == steps - 1)
        def _():
            hl_ref[pl.ds(m * tm, tm), :] = out_ref[...].T

        @pl.when(stage == last)
        def _():
            eps = dot(wout_t[...], out_ref[...])
            x_next = alpha_ref[t] * x_f32[m] + beta_ref[t] * eps
            x_f32[m] = x_next

            @pl.when(t < steps - 1)
            def _():
                x_in[t + 1, m] = x_next.astype(BF16)
                for dev in (5, 3, 1, 4, 2, 0, 6):
                    x_copy(t, m, dev).start()

            @pl.when(t == steps - 1)
            def _():
                x_fin[m] = x_next
                for dev in (5, 3, 1, 4, 2, 0, 6):
                    f_copy(m, dev).start()
        return carry

    lax.fori_loop(0, steps * micro, slot_body, 0)

    def finish_body(m, carry):
        @pl.when(stage < last)
        def _():
            f_copy(m, 0).wait_recv()
            for t in range(steps - 1):
                h_copy(t, m).wait_send()

        @pl.when(stage == last)
        def _():
            for dev in range(last):
                f_copy(m, dev).wait_send()
                for t in range(steps - 1):
                    x_copy(t, m, dev).wait_send()
        xo_ref[pl.ds(m * tm, tm), :] = x_fin[m].T
        return carry
    lax.fori_loop(0, micro, finish_body, 0)


def solution(mesh):
    stages = mesh.shape['stage']

    def stage_program(x_init, h_warm, w_lat, w_qkv, w_o, w_up, w_down, w_out, ada_mods, alpha_coef, beta_coef):
        batch, tokens, ch = x_init.shape
        total = batch * tokens
        steps, heads, head_dim, dim = ada_mods.shape[0], w_o.shape[1], w_o.shape[2], w_o.shape[3]
        hidden = w_up.shape[2]
        micro, tm = MICRO, total // MICRO
        dims = (steps, stages, heads, head_dim, dim, micro, tm)
        any_spec = pl.BlockSpec(memory_space=pl.ANY)
        vmem_spec = pl.BlockSpec(memory_space=pltpu.VMEM)
        smem_spec = pl.BlockSpec(memory_space=pltpu.SMEM)
        x_out, h_last = pl.pallas_call(
            functools.partial(kernel, dims),
            out_shape=(jax.ShapeDtypeStruct((total, ch), F32), jax.ShapeDtypeStruct((total, dim), BF16)),
            in_specs=[any_spec] * 8 + [vmem_spec, smem_spec, smem_spec],
            out_specs=(vmem_spec, vmem_spec),
            scratch_shapes=[
                pltpu.VMEM((ch, dim), BF16), pltpu.VMEM((dim, 3 * dim), BF16), pltpu.VMEM((dim, dim), BF16),
                pltpu.VMEM((dim, hidden), BF16), pltpu.VMEM((hidden, dim), BF16), pltpu.VMEM((dim, ch), BF16),
                pltpu.VMEM((total, dim), BF16), pltpu.VMEM((total, ch), F32),
                pltpu.VMEM((dim, ch), BF16), pltpu.VMEM((3 * dim, dim), BF16), pltpu.VMEM((dim, dim), BF16),
                pltpu.VMEM((hidden, dim), BF16), pltpu.VMEM((dim, hidden), BF16), pltpu.VMEM((ch, dim), BF16),
                pltpu.VMEM((steps, 6, dim, TILE), F32),
                pltpu.VMEM((dim, tm), F32), pltpu.VMEM((dim, tm), BF16), pltpu.VMEM((3 * dim, tm), BF16),
                pltpu.VMEM((dim, tm), BF16), pltpu.VMEM((hidden, tm), BF16), pltpu.VMEM((dim, tm), BF16),
                pltpu.VMEM((steps, micro, dim, tm), BF16), pltpu.VMEM((steps, micro, ch, tm), BF16),
                pltpu.VMEM((steps - 1, micro, dim, tm), BF16), pltpu.VMEM((micro, ch, tm), F32), pltpu.VMEM((micro, ch, tm), F32),
                pltpu.SemaphoreType.DMA((8,)),
                pltpu.SemaphoreType.DMA((steps - 1, micro)), pltpu.SemaphoreType.DMA((steps - 1, micro)),
                pltpu.SemaphoreType.DMA((steps - 1, micro, stages)), pltpu.SemaphoreType.DMA((steps - 1, micro)),
                pltpu.SemaphoreType.DMA((micro, stages)), pltpu.SemaphoreType.DMA((micro,)),
            ],
            compiler_params=pltpu.CompilerParams(collective_id=0, has_side_effects=True, vmem_limit_bytes=60 * 1024 * 1024),
        )(x_init.reshape(total, ch), h_warm.reshape(stages - 1, total, dim), w_lat.reshape(ch, dim),
          w_qkv.reshape(dim, 3 * dim), w_o.reshape(heads * head_dim, dim), w_up.reshape(dim, hidden),
          w_down.reshape(hidden, dim), w_out, ada_mods.reshape(steps, 6, dim), alpha_coef, beta_coef)
        return x_out.reshape(batch, tokens, ch), h_last.reshape(1, batch, tokens, dim)

    return jax.shard_map(stage_program, mesh=mesh,
                         in_specs=(P('data'), P(None, 'data'), P('stage'), P('stage'), P('stage'), P('stage'), P('stage'), P(), P(None, 'stage'), P(), P()),
                         out_specs=(P('data'), P('stage', 'data')), check_vma=False)
```

profile of v0, /device:TPU:0, one launch (start us, length us, event | category | flops | bytes accessed | tf_op | source)
XLA Modules:
  0.0 110.0 jit_solution(9532192675373089764)
XLA Ops:
  0.6 0.8 copy.18
  1.4 0.6 copy.16.mods_ref
  2.0 1.5 %copy.15.wout_hbm = bf16[384,64]{1,0:T(8,128)(2,1)} copy(bf16[384,64]{0,1:T(8,128)(2,1)} %param.18) | data formatting | bytes 98304 | tf_op args[7]
  3.6 102.8 %shard_map.122 = (f32[2048,64]{1,0:T(8,128)}, bf16[2048,384]{1,0:T(8,128)(2,1)}) custom-call(f32[2048,64]{1,0:T(8,128)} %bitcast.16, bf16[7,2048,384]{2,1,0:T(8,128)(2,1)} %bitcast.12, bf16[64,384]{1,0:T(8,128)(2,1)} %bitcast.21, bf16[384,1152]{1,0:T(8,128)(2,1)} %bitcast.18, bf16[384,384]{1,0:T(8,128)(2,1)} %bitcast.19, bf16[384,1536]{1,0:T(8,128)(2,1)} %bitcast.14, ...), custom_call_target="tpu_custom_call" | custom-call | tf_op jit(solution)/shard_map/pallas_call | solution.py:236
  106.4 0.0 copy-start
  106.4 2.4 %copy.21 = f32[32,64,64]{2,1,0:T(8,128)} copy(f32[32,64,64]{2,1,0:T(8,128)} %bitcast.17) | data formatting | bytes 1048576
  108.8 0.0 copy-done
  108.8 1.1 %copy.22 = bf16[1,32,64,384]{3,2,1,0:T(8,128)(2,1)} copy(bf16[1,32,64,384]{3,2,1,0:T(8,128)(2,1)S(1)} %bitcast.13) | data formatting | bytes 3145728
Async XLA Ops:
  106.4 2.4 %copy-start = (bf16[2048,384]{1,0:T(8,128)(2,1)S(1)}, bf16[2048,384]{1,0:T(8,128)(2,1)}, u32[]{:S(2)}) copy-start(bf16[2048,384]{1,0:T(8,128)(2,1)} %get-tuple-element.5) | copy-start | bytes 4718596
where the time goes:
time: 110 us
  Pallas kernels  103 us (94%)
  local copies, waits for them, and re-layouts  6.52 us (6%)
    pallas_call x1, Pallas kernels, stage_program(): pl.pallas_call(functools.partial(kernel, dims), out_shape=(jax.ShapeDtype...  103 us
    unnamed x6, local copies, waits for them, and re-layouts  5.89 us

commit v1 on v0

v1 whole, which is shorter than its diff:
```python
import functools
import math

import jax
import jax.numpy as jnp
from jax import lax
from jax.experimental import pallas as pl
from jax.experimental.pallas import tpu as pltpu
from jax.sharding import PartitionSpec as P

MESH = pl.DeviceIdType.MESH
F32, BF16 = jnp.float32, jnp.bfloat16
GROUP = 256
TILE = 128
GELU_A = math.sqrt(2.0 / math.pi)
GELU_B = 0.044715


def dot(lhs, rhs):
    return lax.dot_general(lhs, rhs, (((1,), (0,)), ((), ())), preferred_element_type=F32)


def layer_norm(h, scale, shift):
    mean = jnp.sum(h, axis=0, keepdims=True) * (1.0 / h.shape[0])
    centered = h - mean
    var = jnp.sum(centered * centered, axis=0, keepdims=True) * (1.0 / h.shape[0])
    return centered * lax.rsqrt(var + 1e-6) * scale + shift


def kernel(dims, x_hbm, warm_hbm, wlat_hbm, wqkv_hbm, wo_hbm, wup_hbm, wdown_hbm, wout_ref, mods_ref, alpha_ref, beta_ref,
           xo_ref, hl_ref,
           wlat_raw, wqkv_raw, wo_raw, wup_raw, wdown_raw, warm_raw, x_raw,
           wlat_t, wqkv_t, wo_t, wup_t, wdown_t, modb,
           h_ref, hb_ref, h2_ref, h2b_ref, u_ref, u2_ref, q_ref, k_ref, v_ref, att_ref, hid_ref,
           b_in, x_in, b_out, x_out, x_f32,
           load_sem, hs_sem, hr_sem, xs_sem, xr_sem, fs_sem, fr_sem):
    steps, stages, heads, head_dim, dim, micro, tm = dims
    stage = lax.axis_index('stage')
    last = stages - 1
    hidden = wup_t.shape[0]
    slots = steps * micro
    others = (5, 3, 1, 4, 2, 0, 6)

    loads = [pltpu.make_async_copy(src, dst, load_sem.at[i]) for i, (src, dst) in enumerate((
        (x_hbm, x_raw), (wlat_hbm, wlat_raw), (wqkv_hbm, wqkv_raw), (wo_hbm, wo_raw),
        (wup_hbm, wup_raw), (wdown_hbm, wdown_raw)))]
    warm = pltpu.make_async_copy(warm_hbm.at[jnp.maximum(stage - 1, 0)], warm_raw, load_sem.at[6])
    for copy in loads:
        copy.start()
    warm.start()

    barrier = pltpu.get_barrier_semaphore()
    for shift in range(1, stages):
        pl.semaphore_signal(barrier, inc=1, device_id={'stage': lax.rem(stage + shift, stages)}, device_id_type=MESH)

    def make_mods(t):
        for i in range(6):
            row = mods_ref[i, pl.ds(t, 1), :]
            if i in (1, 4):
                row = row + 1.0
            modb[t, i] = jnp.broadcast_to(row, (TILE, dim)).T

    def make_inputs(m):
        xt = x_raw[pl.ds(m * tm, tm), :].T
        x_f32[m] = xt
        x_in[0, m] = xt.astype(BF16)

        @pl.when(stage > 0)
        def _():
            b_in[0, m] = warm_raw[pl.ds(m * tm, tm), :].T

        @pl.when(stage == 0)
        def _():
            for t in range(steps):
                b_in[t, m] = jnp.zeros((dim, tm), BF16)

    make_mods(0)
    loads[0].wait()
    warm.wait()
    make_inputs(0)
    for copy in loads[1:3]:
        copy.wait()
    wlat_t[...] = wlat_raw[...].T
    wqkv_t[...] = wqkv_raw[...].T
    for copy in loads[3:]:
        copy.wait()

    def late_weights():
        wo_t[...] = wo_raw[...].T
        for j in range(hidden // dim):
            wup_t[j * dim:(j + 1) * dim, :] = wup_raw[:, j * dim:(j + 1) * dim].T * jnp.asarray(0.5, BF16)
            wdown_t[:, j * dim:(j + 1) * dim] = wdown_raw[j * dim:(j + 1) * dim, :].T

    def h_copy(t, m):
        return pltpu.make_async_remote_copy(
            src_ref=b_out.at[t, m], dst_ref=b_in.at[t + 1, m], send_sem=hs_sem, recv_sem=hr_sem.at[t, m],
            device_id={'stage': jnp.minimum(stage + 1, last)}, device_id_type=MESH)

    def x_copy(t, m, dev):
        return pltpu.make_async_remote_copy(
            src_ref=x_out.at[t, m], dst_ref=x_in.at[t + 1, m], send_sem=xs_sem.at[dev], recv_sem=xr_sem.at[t, m],
            device_id={'stage': dev}, device_id_type=MESH)

    def f_copy(m, src, dev):
        return pltpu.make_async_remote_copy(
            src_ref=src.at[m], dst_ref=xo_ref.at[m], send_sem=fs_sem.at[dev], recv_sem=fr_sem,
            device_id={'stage': dev}, device_id_type=MESH)

    low_half = lax.rem(lax.broadcasted_iota(jnp.int32, (head_dim, 2 * TILE), 1), TILE) < head_dim
    score_scale = head_dim ** -0.5 * math.log2(math.e)
    tiles = [slice(i * TILE, (i + 1) * TILE) for i in range(tm // TILE)]
    halves = [slice(0, dim // 2), slice(dim // 2, dim)]
    zero_q = jnp.zeros((head_dim, TILE), BF16)
    zero_p = jnp.zeros((TILE, TILE), BF16)

    def step_of(slot):
        return lax.div(slot, micro), lax.rem(slot, micro)

    def attn_in(slot):
        t, m = step_of(slot)
        for rows in halves:
            h_ref[rows, :] = b_in[t, m, rows, :].astype(F32) + dot(wlat_t[rows, :], x_in[t, m])

    def attn_norm(slot):
        t, _ = step_of(slot)
        for tile in tiles:
            u_ref[:, tile] = layer_norm(h_ref[:, tile], modb[t, 1], modb[t, 0]).astype(BF16)

    def project(part, dst):
        for rows in halves:
            dst[rows, :] = dot(wqkv_t[part * dim + rows.start:part * dim + rows.stop, :], u_ref[...]).astype(BF16)

    def score_dots():
        scores = []
        for hp in range(heads // 2):
            rows = slice(hp * TILE, (hp + 1) * TILE)
            q_pair = q_ref[rows, :]
            k_pair = k_ref[rows, :].T
            for span in tiles:
                q_blk = jnp.concatenate([
                    jnp.concatenate([q_pair[:head_dim, span], zero_q], axis=1),
                    jnp.concatenate([zero_q, q_pair[head_dim:, span]], axis=1)], axis=0)
                full = dot(k_pair[span, :], q_blk)
                scores.append(jnp.where(low_half, full[:head_dim], full[head_dim:]))
        return scores

    def softmax(scores):
        top = jnp.max(scores, axis=0, keepdims=True)
        expd = jnp.exp2((scores - top) * score_scale)
        prob = expd * (1.0 / jnp.sum(expd, axis=0, keepdims=True))
        return jnp.concatenate([jnp.where(low_half, prob, 0.0).astype(BF16), jnp.where(low_half, 0.0, prob).astype(BF16)], axis=0)

    def value_dots(probs):
        for head in range(heads):
            hp, span = head // 2, tiles[head % 2]
            p_blk = jnp.concatenate([
                jnp.concatenate([probs[2 * hp][:, span], zero_p], axis=1),
                jnp.concatenate([zero_p, probs[2 * hp + 1][:, span]], axis=1)], axis=0)
            rows = slice(head * head_dim, (head + 1) * head_dim)
            att_ref[rows, :] = dot(v_ref[rows, :], p_blk).astype(BF16)

    def attn_out(slot):
        t, _ = step_of(slot)
        for rows in halves:
            proj = dot(wo_t[rows, :], att_ref[...])
            for tile in tiles:
                h2_ref[rows, tile] = hb_ref[rows, tile] + modb[t, 2, rows, :] * proj[:, tile]

    def mlp_norm(slot):
        t, _ = step_of(slot)
        for tile in tiles:
            u2_ref[:, tile] = layer_norm(h2_ref[:, tile], modb[t, 4], modb[t, 3]).astype(BF16)

    def mlp_up(j):
        rows = slice(j * GROUP, (j + 1) * GROUP)
        half = dot(wup_t[rows, :], u2_ref[...])
        inner = half * (half * half * (8.0 * GELU_A * GELU_B) + 2.0 * GELU_A)
        hid_ref[rows, :] = (half + half * jnp.tanh(inner)).astype(BF16)

    def mlp_down(slot, part):
        t, m = step_of(slot)
        cut = slice(part * hidden // 2, (part + 1) * hidden // 2)
        for rows in halves:
            down = dot(wdown_t[rows, cut], hid_ref[cut, :])
            for tile in tiles:
                if part == 0:
                    h2b_ref[rows, tile] = h2b_ref[rows, tile] + modb[t, 5, rows, :] * down[:, tile]
                else:
                    b_out[t, m, rows, tile] = (h2b_ref[rows, tile] + modb[t, 5, rows, :] * down[:, tile]).astype(BF16)

    def latent(slot):
        t, m = step_of(slot)
        eps = dot(wout_ref[...], b_out[t, m])
        x_next = alpha_ref[t] * x_f32[m] + beta_ref[t] * eps
        x_f32[m] = x_next
        x_out[t, m] = x_next.astype(BF16)
        hl_ref[pl.ds(m * tm, tm), :] = b_out[t, m].T

    def receive(slot):
        t, m = step_of(slot)

        @pl.when(jnp.logical_and(t > 0, stage > 0))
        def _():
            h_copy(t - 1, m).wait_recv()

        @pl.when(jnp.logical_and(t > 0, stage < last))
        def _():
            x_copy(t - 1, m, 0).wait_recv()

    def send_stage(slot):
        t, m = step_of(slot)

        @pl.when(jnp.logical_and(t < steps - 1, stage < last))
        def _():
            h_copy(t, m).start()

    def send_latent(slot):
        t, m = step_of(slot)

        @pl.when(jnp.logical_and(t < steps - 1, stage == last))
        def _():
            x_in[t + 1, m] = x_out[t, m]
            for dev in others:
                x_copy(t, m, dev).start()

        @pl.when(jnp.logical_and(t == steps - 1, stage == last))
        def _():
            xo_ref[m] = x_f32[m]
            for dev in (5, 3, 1, 6):
                f_copy(m, x_f32, dev).start()

    def block(attn=None, out=None, mlp=None, lat=None, extra=None):
        ups = hidden // GROUP
        if mlp is not None:
            h2b_ref[...] = h2_ref[...]
        if out is not None:
            hb_ref[...] = h_ref[...]
        if attn is not None:
            attn_in(attn)
        if lat is not None:
            latent(lat)
        if mlp is not None:
            for j in range(4):
                mlp_up(j)
        if attn is not None:
            attn_norm(attn)
            project(0, q_ref)
            project(1, k_ref)
        if mlp is not None:
            for j in range(4, ups):
                mlp_up(j)
        if attn is not None:
            scores = score_dots()
            project(2, v_ref)
        if out is not None:
            attn_out(out)
            mlp_norm(out)
        if extra is not None:
            extra()
        if mlp is not None:
            mlp_down(mlp, 0)
        if attn is not None:
            value_dots([softmax(s) for s in scores])
        if mlp is not None:
            mlp_down(mlp, 1)
            send_stage(mlp)
        if lat is not None:
            send_latent(lat)

    def whole_slot(slot):
        receive(slot)
        attn_in(slot)
        attn_norm(slot)
        project(0, q_ref)
        project(1, k_ref)
        scores = score_dots()
        project(2, v_ref)
        hb_ref[...] = h_ref[...]
        value_dots([softmax(s) for s in scores])
        attn_out(slot)
        mlp_norm(slot)
        h2b_ref[...] = h2_ref[...]
        for j in range(hidden // GROUP):
            mlp_up(j)
        mlp_down(slot, 0)
        mlp_down(slot, 1)
        latent(slot)
        send_latent(slot)

    block(attn=0, extra=late_weights)
    make_inputs(1)
    block(attn=1, out=0)
    make_inputs(2)
    pl.semaphore_wait(barrier, stages - 1)

    def slot_body(slot, carry):
        t, m = step_of(slot)
        receive(slot)
        block(slot, slot - 1, slot - 2, slot - 3)

        @pl.when(slot + 1 < micro)
        def _():
            make_inputs(slot + 1)

        @pl.when(jnp.logical_and(m == micro - 1, t < steps - 1))
        def _():
            make_mods(t + 1)
        return carry
    block(2, 1, 0)
    make_inputs(3)
    tail = slots - 2
    lax.fori_loop(3, tail, slot_body, 0)
    block(None, tail - 1, tail - 2, tail - 3)
    block(None, None, tail - 1, tail - 2)
    block(None, None, None, tail - 1)

    def tail_body(slot, carry):
        whole_slot(slot)
        return carry
    lax.fori_loop(tail, slots, tail_body, 0)

    def whole(src, dst, sem, dev):
        return pltpu.make_async_remote_copy(
            src_ref=src, dst_ref=dst, send_sem=sem, recv_sem=fr_sem, device_id={'stage': dev}, device_id_type=MESH)

    sent = pl.ds(0, steps - 1)

    @pl.when(stage < last)
    def _():
        whole(xo_ref, xo_ref, fs_sem.at[0], 0).wait_recv()
    for src, dev in ((5, 4), (3, 2), (1, 0)):
        @pl.when(stage == src)
        def _(dev=dev):
            whole(xo_ref, xo_ref, fs_sem.at[dev], dev).start()

    @pl.when(stage < last)
    def _():
        whole(b_out.at[sent], b_in.at[pl.ds(1, steps - 1)], hs_sem, jnp.minimum(stage + 1, last)).wait_send()
    for src, dev in ((5, 4), (3, 2), (1, 0)):
        @pl.when(stage == src)
        def _(dev=dev):
            whole(xo_ref, xo_ref, fs_sem.at[dev], dev).wait_send()

    @pl.when(stage == last)
    def _():
        for dev in others:
            whole(x_out.at[sent], x_in.at[pl.ds(1, steps - 1)], xs_sem.at[dev], dev).wait_send()
        for dev in (5, 3, 1, 6):
            whole(x_f32, xo_ref, fs_sem.at[dev], dev).wait_send()


def solution(mesh):
    stages = mesh.shape['stage']

    def stage_program(x_init, h_warm, w_lat, w_qkv, w_o, w_up, w_down, w_out, ada_mods, alpha_coef, beta_coef):
        batch, tokens, ch = x_init.shape
        total = batch * tokens
        steps, heads, head_dim, dim = ada_mods.shape[0], w_o.shape[1], w_o.shape[2], w_o.shape[3]
        hidden = w_up.shape[2]
        micro, tm = total // GROUP, GROUP
        dims = (steps, stages, heads, head_dim, dim, micro, tm)
        any_spec = pl.BlockSpec(memory_space=pl.ANY)
        vmem_spec = pl.BlockSpec(memory_space=pltpu.VMEM)
        smem_spec = pl.BlockSpec(memory_space=pltpu.SMEM)
        x_out, h_last = pl.pallas_call(
            functools.partial(kernel, dims),
            out_shape=(jax.ShapeDtypeStruct((micro, ch, tm), F32), jax.ShapeDtypeStruct((total, dim), BF16)),
            in_specs=[any_spec] * 7 + [vmem_spec, vmem_spec, smem_spec, smem_spec],
            out_specs=(vmem_spec, vmem_spec),
            scratch_shapes=[
                pltpu.VMEM((ch, dim), BF16), pltpu.VMEM((dim, 3 * dim), BF16), pltpu.VMEM((dim, dim), BF16),
                pltpu.VMEM((dim, hidden), BF16), pltpu.VMEM((hidden, dim), BF16),
                pltpu.VMEM((total, dim), BF16), pltpu.VMEM((total, ch), F32),
                pltpu.VMEM((dim, ch), BF16), pltpu.VMEM((3 * dim, dim), BF16), pltpu.VMEM((dim, dim), BF16),
                pltpu.VMEM((hidden, dim), BF16), pltpu.VMEM((dim, hidden), BF16),
                pltpu.VMEM((steps, 6, dim, TILE), F32),
                pltpu.VMEM((dim, tm), F32), pltpu.VMEM((dim, tm), F32), pltpu.VMEM((dim, tm), F32), pltpu.VMEM((dim, tm), F32),
                pltpu.VMEM((dim, tm), BF16), pltpu.VMEM((dim, tm), BF16),
                pltpu.VMEM((dim, tm), BF16), pltpu.VMEM((dim, tm), BF16), pltpu.VMEM((dim, tm), BF16),
                pltpu.VMEM((dim, tm), BF16), pltpu.VMEM((hidden, tm), BF16),
                pltpu.VMEM((steps, micro, dim, tm), BF16), pltpu.VMEM((steps, micro, ch, tm), BF16),
                pltpu.VMEM((steps, micro, dim, tm), BF16), pltpu.VMEM((steps, micro, ch, tm), BF16), pltpu.VMEM((micro, ch, tm), F32),
                pltpu.SemaphoreType.DMA((7,)),
                pltpu.SemaphoreType.DMA, pltpu.SemaphoreType.DMA((steps - 1, micro)),
                pltpu.SemaphoreType.DMA((stages,)), pltpu.SemaphoreType.DMA((steps - 1, micro)),
                pltpu.SemaphoreType.DMA((stages,)), pltpu.SemaphoreType.DMA,
            ],
            compiler_params=pltpu.CompilerParams(collective_id=0, has_side_effects=True, vmem_limit_bytes=60 * 1024 * 1024),
        )(x_init.reshape(total, ch), h_warm.reshape(stages - 1, total, dim), w_lat.reshape(ch, dim),
          w_qkv.reshape(dim, 3 * dim), w_o.reshape(heads * head_dim, dim), w_up.reshape(dim, hidden),
          w_down.reshape(hidden, dim), w_out.T, ada_mods.reshape(steps, 6, dim).transpose(1, 0, 2), alpha_coef, beta_coef)
        x_out = x_out.transpose(0, 2, 1)
        return x_out.reshape(batch, tokens, ch), h_last.reshape(1, batch, tokens, dim)

    return jax.shard_map(stage_program, mesh=mesh,
                         in_specs=(P('data'), P(None, 'data'), P('stage'), P('stage'), P('stage'), P('stage'), P('stage'), P(), P(None, 'stage'), P(), P()),
                         out_specs=(P('data'), P('stage', 'data')), check_vma=False)
```

time: 110 us -> 83.2 us (0.76)
  Pallas kernels: 103 us -> 77.3 us
  local copies, waits for them, and re-layouts: 6.52 us -> 5.01 us
    pallas_call x1, Pallas kernels: 103 us -> 77.3 us  [stage_program(): pl.pallas_call(functools.partial(kernel, dims), out_shape=(jax.ShapeDtype...]
    unnamed x6 -> x5, local copies, waits for them, and re-layouts: 5.89 us -> 5.01 us
where the time goes in v1:
time: 83.2 us; the launch traced here: 83 us
  Pallas kernels  77.3 us (93%)
  local copies, waits for them, and re-layouts  5.01 us (6%)
    pallas_call x1, Pallas kernels, stage_program(): pl.pallas_call(functools.partial(kernel, dims), out_shape=(jax.ShapeDtype...  77.3 us
    unnamed x5, local copies, waits for them, and re-layouts  5.01 us

profile of v1, /device:TPU:0, one launch (start us, length us, event | category | flops | bytes accessed | tf_op | source)
XLA Modules:
  0.0 83.0 jit_solution(3602272808208421889)
XLA Ops:
  0.6 1.4 %copy.20 = f32[4,1,6,384]{3,0,2,1:T(4,128)} copy(f32[4,1,6,384]{3,1,2,0:T(1,128)} %param.19) | data formatting | bytes 73728 | tf_op args[8]
  2.0 77.3 %shard_map.122 = (f32[8,64,256]{2,1,0:T(8,128)}, bf16[2048,384]{1,0:T(8,128)(2,1)}) custom-call(f32[2048,64]{1,0:T(8,128)} %bitcast.20, bf16[7,2048,384]{2,1,0:T(8,128)(2,1)} %bitcast.16, bf16[64,384]{1,0:T(8,128)(2,1)} %bitcast.26, bf16[384,1152]{1,0:T(8,128)(2,1)} %bitcast.22, bf16[384,384]{1,0:T(8,128)(2,1)} %bitcast.24, bf16[384,1536]{1,0:T(8,128)(2,1)} %bitcast.18, ...), custom_call_target="tpu_custom_call" | custom-call | tf_op jit(solution)/shard_map/pallas_call | solution.py:365
  79.3 0.0 copy-start
  79.3 2.5 %copy.17 = f32[8,256,64]{2,1,0:T(8,128)} copy(f32[8,256,64]{1,2,0:T(8,128)} %bitcast.23) | data formatting | bytes 1048576
  81.8 0.0 copy-done
  81.8 1.1 %copy.22 = bf16[1,32,64,384]{3,2,1,0:T(8,128)(2,1)} copy(bf16[1,32,64,384]{3,2,1,0:T(8,128)(2,1)S(1)} %bitcast.17) | data formatting | bytes 3145728
Async XLA Ops:
  79.3 2.5 %copy-start = (bf16[2048,384]{1,0:T(8,128)(2,1)S(1)}, bf16[2048,384]{1,0:T(8,128)(2,1)}, u32[]{:S(2)}) copy-start(bf16[2048,384]{1,0:T(8,128)(2,1)} %get-tuple-element.5) | copy-start | bytes 4718596

commit v2 on v1

--- a/solution.py
+++ b/solution.py
@@ -20,16 +20,26 @@
     return lax.dot_general(lhs, rhs, (((1,), (0,)), ((), ())), preferred_element_type=F32)
 
 
-def layer_norm(h, scale, shift):
-    mean = jnp.sum(h, axis=0, keepdims=True) * (1.0 / h.shape[0])
-    centered = h - mean
-    var = jnp.sum(centered * centered, axis=0, keepdims=True) * (1.0 / h.shape[0])
-    return centered * lax.rsqrt(var + 1e-6) * scale + shift
-
-
-def kernel(dims, x_hbm, warm_hbm, wlat_hbm, wqkv_hbm, wo_hbm, wup_hbm, wdown_hbm, wout_ref, mods_ref, alpha_ref, beta_ref,
+def layer_norm(src, dst, scale, shift):
+    dim, tm = src.shape
+    chunks = [slice(i, i + 64) for i in range(0, dim, 64)]
+
+    def total(terms):
+        part = sum(jnp.sum(term.reshape(8, 8, tm), axis=0) for term in terms)
+        return jnp.sum(part, axis=0, keepdims=True) * (1.0 / dim)
+
+    mean = total(src[rows, :] for rows in chunks)
+    var = total((src[rows, :] - mean) * (src[rows, :] - mean) for rows in chunks)
+    inv = lax.rsqrt(var + 1e-6)
+    for rows in chunks:
+        for lane in range(0, tm, TILE):
+            tile = slice(lane, lane + TILE)
+            dst[rows, tile] = ((src[rows, tile] - mean[:, tile]) * inv[:, tile] * scale[rows, :] + shift[rows, :]).astype(BF16)
+
+
+def kernel(dims, x_hbm, warm_hbm, wlat_hbm, wqkv_hbm, wo_hbm, wup_hbm, wdown_hbm, wout_hbm, mods_hbm, alpha_ref, beta_ref,
            xo_ref, hl_ref,
-           wlat_raw, wqkv_raw, wo_raw, wup_raw, wdown_raw, warm_raw, x_raw,
+           wout_ref, mods_ref, wlat_raw, wqkv_raw, wo_raw, wup_raw, wdown_raw, warm_raw, x_raw,
            wlat_t, wqkv_t, wo_t, wup_t, wdown_t, modb,
            h_ref, hb_ref, h2_ref, h2b_ref, u_ref, u2_ref, q_ref, k_ref, v_ref, att_ref, hid_ref,
            b_in, x_in, b_out, x_out, x_f32,
@@ -43,11 +53,14 @@
 
     loads = [pltpu.make_async_copy(src, dst, load_sem.at[i]) for i, (src, dst) in enumerate((
         (x_hbm, x_raw), (wlat_hbm, wlat_raw), (wqkv_hbm, wqkv_raw), (wo_hbm, wo_raw),
-        (wup_hbm, wup_raw), (wdown_hbm, wdown_raw)))]
-    warm = pltpu.make_async_copy(warm_hbm.at[jnp.maximum(stage - 1, 0)], warm_raw, load_sem.at[6])
-    for copy in loads:
+        (wup_hbm, wup_raw), (wdown_hbm, wdown_raw), (wout_hbm, wout_ref)))]
+    mods = pltpu.make_async_copy(mods_hbm, mods_ref, load_sem.at[8])
+    warm = pltpu.make_async_copy(warm_hbm.at[jnp.maximum(stage - 1, 0)], warm_raw, load_sem.at[7])
+    mods.start()
+    loads[0].start()
+    warm.start()
+    for copy in loads[1:]:
         copy.start()
-    warm.start()
 
     barrier = pltpu.get_barrier_semaphore()
     for shift in range(1, stages):
@@ -55,10 +68,11 @@
 
     def make_mods(t):
         for i in range(6):
-            row = mods_ref[i, pl.ds(t, 1), :]
-            if i in (1, 4):
-                row = row + 1.0
-            modb[t, i] = jnp.broadcast_to(row, (TILE, dim)).T
+            for c in range(dim // TILE):
+                row = mods_ref[pl.ds((t * 6 + i) * (dim // TILE) + c, 1), :]
+                if i in (1, 4):
+                    row = row + 1.0
+                modb[t, i, c * TILE:(c + 1) * TILE, :] = jnp.broadcast_to(row, (TILE, TILE)).T
 
     def make_inputs(m):
         xt = x_raw[pl.ds(m * tm, tm), :].T
@@ -74,10 +88,19 @@
             for t in range(steps):
                 b_in[t, m] = jnp.zeros((dim, tm), BF16)
 
-    make_mods(0)
+    mods.wait()
+
+    def mods_body(t, carry):
+        make_mods(t)
+        return carry
+    lax.fori_loop(0, steps, mods_body, 0)
     loads[0].wait()
     warm.wait()
-    make_inputs(0)
+
+    def inputs_body(m, carry):
+        make_inputs(m)
+        return carry
+    lax.fori_loop(0, micro, inputs_body, 0)
     for copy in loads[1:3]:
         copy.wait()
     wlat_t[...] = wlat_raw[...].T
@@ -123,8 +146,7 @@
 
     def attn_norm(slot):
         t, _ = step_of(slot)
-        for tile in tiles:
-            u_ref[:, tile] = layer_norm(h_ref[:, tile], modb[t, 1], modb[t, 0]).astype(BF16)
+        layer_norm(h_ref, u_ref, modb.at[t, 1], modb.at[t, 0])
 
     def project(part, dst):
         for rows in halves:
@@ -147,8 +169,9 @@
     def softmax(scores):
         top = jnp.max(scores, axis=0, keepdims=True)
         expd = jnp.exp2((scores - top) * score_scale)
-        prob = expd * (1.0 / jnp.sum(expd, axis=0, keepdims=True))
-        return jnp.concatenate([jnp.where(low_half, prob, 0.0).astype(BF16), jnp.where(low_half, 0.0, prob).astype(BF16)], axis=0)
+        prob = (expd * (1.0 / jnp.sum(expd, axis=0, keepdims=True))).astype(BF16)
+        nought = jnp.zeros_like(prob)
+        return jnp.concatenate([jnp.where(low_half, prob, nought), jnp.where(low_half, nought, prob)], axis=0)
 
     def value_dots(probs):
         for head in range(heads):
@@ -168,8 +191,7 @@
 
     def mlp_norm(slot):
         t, _ = step_of(slot)
-        for tile in tiles:
-            u2_ref[:, tile] = layer_norm(h2_ref[:, tile], modb[t, 4], modb[t, 3]).astype(BF16)
+        layer_norm(h2_ref, u2_ref, modb.at[t, 4], modb.at[t, 3])
 
     def mlp_up(j):
         rows = slice(j * GROUP, (j + 1) * GROUP)
@@ -184,7 +206,7 @@
             down = dot(wdown_t[rows, cut], hid_ref[cut, :])
             for tile in tiles:
                 if part == 0:
-                    h2b_ref[rows, tile] = h2b_ref[rows, tile] + modb[t, 5, rows, :] * down[:, tile]
+                    h2b_ref[rows, tile] = h2_ref[rows, tile] + modb[t, 5, rows, :] * down[:, tile]
                 else:
                     b_out[t, m, rows, tile] = (h2b_ref[rows, tile] + modb[t, 5, rows, :] * down[:, tile]).astype(BF16)
 
@@ -231,8 +253,6 @@
 
     def block(attn=None, out=None, mlp=None, lat=None, extra=None):
         ups = hidden // GROUP
-        if mlp is not None:
-            h2b_ref[...] = h2_ref[...]
         if out is not None:
             hb_ref[...] = h_ref[...]
         if attn is not None:
@@ -252,13 +272,13 @@
         if attn is not None:
             scores = score_dots()
             project(2, v_ref)
+        if mlp is not None:
+            mlp_down(mlp, 0)
         if out is not None:
             attn_out(out)
             mlp_norm(out)
         if extra is not None:
             extra()
-        if mlp is not None:
-            mlp_down(mlp, 0)
         if attn is not None:
             value_dots([softmax(s) for s in scores])
         if mlp is not None:
@@ -267,57 +287,20 @@
         if lat is not None:
             send_latent(lat)
 
-    def whole_slot(slot):
-        receive(slot)
-        attn_in(slot)
-        attn_norm(slot)
-        project(0, q_ref)
-        project(1, k_ref)
-        scores = score_dots()
-        project(2, v_ref)
-        hb_ref[...] = h_ref[...]
-        value_dots([softmax(s) for s in scores])
-        attn_out(slot)
-        mlp_norm(slot)
-        h2b_ref[...] = h2_ref[...]
-        for j in range(hidden // GROUP):
-            mlp_up(j)
-        mlp_down(slot, 0)
-        mlp_down(slot, 1)
-        latent(slot)
-        send_latent(slot)
-
     block(attn=0, extra=late_weights)
-    make_inputs(1)
     block(attn=1, out=0)
-    make_inputs(2)
     pl.semaphore_wait(barrier, stages - 1)
 
     def slot_body(slot, carry):
         t, m = step_of(slot)
         receive(slot)
         block(slot, slot - 1, slot - 2, slot - 3)
-
-        @pl.when(slot + 1 < micro)
-        def _():
-            make_inputs(slot + 1)
-
-        @pl.when(jnp.logical_and(m == micro - 1, t < steps - 1))
-        def _():
-            make_mods(t + 1)
         return carry
     block(2, 1, 0)
-    make_inputs(3)
-    tail = slots - 2
-    lax.fori_loop(3, tail, slot_body, 0)
-    block(None, tail - 1, tail - 2, tail - 3)
-    block(None, None, tail - 1, tail - 2)
-    block(None, None, None, tail - 1)
-
-    def tail_body(slot, carry):
-        whole_slot(slot)
-        return carry
-    lax.fori_loop(tail, slots, tail_body, 0)
+    lax.fori_loop(3, slots, slot_body, 0)
+    block(None, slots - 1, slots - 2, slots - 3)
+    block(None, None, slots - 1, slots - 2)
+    block(None, None, None, slots - 1)
 
     def whole(src, dst, sem, dev):
         return pltpu.make_async_remote_copy(
@@ -364,10 +347,11 @@
         smem_spec = pl.BlockSpec(memory_space=pltpu.SMEM)
         x_out, h_last = pl.pallas_call(
             functools.partial(kernel, dims),
-            out_shape=(jax.ShapeDtypeStruct((micro, ch, tm), F32), jax.ShapeDtypeStruct((total, dim), BF16)),
-            in_specs=[any_spec] * 7 + [vmem_spec, vmem_spec, smem_spec, smem_spec],
+            out_shape=(pltpu.VMEM((micro, ch, tm), F32), pltpu.VMEM((total, dim), BF16)),
+            in_specs=[any_spec] * 9 + [smem_spec, smem_spec],
             out_specs=(vmem_spec, vmem_spec),
             scratch_shapes=[
+                pltpu.VMEM((ch, dim), BF16), pltpu.VMEM((steps * 6 * dim // TILE, TILE), F32),
                 pltpu.VMEM((ch, dim), BF16), pltpu.VMEM((dim, 3 * dim), BF16), pltpu.VMEM((dim, dim), BF16),
                 pltpu.VMEM((dim, hidden), BF16), pltpu.VMEM((hidden, dim), BF16),
                 pltpu.VMEM((total, dim), BF16), pltpu.VMEM((total, ch), F32),
@@ -380,7 +364,7 @@
                 pltpu.VMEM((dim, tm), BF16), pltpu.VMEM((hidden, tm), BF16),
                 pltpu.VMEM((steps, micro, dim, tm), BF16), pltpu.VMEM((steps, micro, ch, tm), BF16),
                 pltpu.VMEM((steps, micro, dim, tm), BF16), pltpu.VMEM((steps, micro, ch, tm), BF16), pltpu.VMEM((micro, ch, tm), F32),
-                pltpu.SemaphoreType.DMA((7,)),
+                pltpu.SemaphoreType.DMA((9,)),
                 pltpu.SemaphoreType.DMA, pltpu.SemaphoreType.DMA((steps - 1, micro)),
                 pltpu.SemaphoreType.DMA((stages,)), pltpu.SemaphoreType.DMA((steps - 1, micro)),
                 pltpu.SemaphoreType.DMA((stages,)), pltpu.SemaphoreType.DMA,
@@ -388,7 +372,7 @@
             compiler_params=pltpu.CompilerParams(collective_id=0, has_side_effects=True, vmem_limit_bytes=60 * 1024 * 1024),
         )(x_init.reshape(total, ch), h_warm.reshape(stages - 1, total, dim), w_lat.reshape(ch, dim),
           w_qkv.reshape(dim, 3 * dim), w_o.reshape(heads * head_dim, dim), w_up.reshape(dim, hidden),
-          w_down.reshape(hidden, dim), w_out.T, ada_mods.reshape(steps, 6, dim).transpose(1, 0, 2), alpha_coef, beta_coef)
+          w_down.reshape(hidden, dim), w_out.T, ada_mods.reshape(steps * 6 * dim // TILE, TILE), alpha_coef, beta_coef)
         x_out = x_out.transpose(0, 2, 1)
         return x_out.reshape(batch, tokens, ch), h_last.reshape(1, batch, tokens, dim)
 

time: 83.2 us -> 78.5 us (0.944)
  local copies, waits for them, and re-layouts: 5.01 us -> 2.45 us
  Pallas kernels: 77.3 us -> 75.3 us
    unnamed x5 -> x2, local copies, waits for them, and re-layouts: 5.01 us -> 2.45 us
    pallas_call x1, Pallas kernels: 77.3 us -> 75.3 us  [stage_program(): pl.pallas_call(functools.partial(kernel, dims), out_shape=(pltpu.VMEM((mi...]
where the time goes in v2:
time: 78.5 us; the launch traced here: 78.4 us
  Pallas kernels  75.3 us (96%)
  local copies, waits for them, and re-layouts  2.45 us (3%)
    pallas_call x1, Pallas kernels, stage_program(): pl.pallas_call(functools.partial(kernel, dims), out_shape=(pltpu.VMEM((mi...  75.3 us
    unnamed x2, local copies, waits for them, and re-layouts  2.45 us

profile of v2, /device:TPU:0, one launch (start us, length us, event | category | flops | bytes accessed | tf_op | source)
XLA Modules:
  0.0 78.4 jit_solution(16878628839909541256)
XLA Ops:
  0.6 75.3 %shard_map.122 = (f32[8,64,256]{2,1,0:T(8,128)S(1)}, bf16[2048,384]{1,0:T(8,128)(2,1)S(1)}) custom-call(f32[2048,64]{1,0:T(8,128)} %bitcast.17, bf16[7,2048,384]{2,1,0:T(8,128)(2,1)} %bitcast.14, bf16[64,384]{1,0:T(8,128)(2,1)} %bitcast.21, bf16[384,1152]{1,0:T(8,128)(2,1)} %bitcast.19, bf16[384,384]{1,0:T(8,128)(2,1)} %bitcast.20, ...), custom_call_target="tpu_custom_call" | custom-call | tf_op jit(solution)/shard_map/pallas_call | solution.py:348
  75.9 1.1 %copy.18 = bf16[1,32,64,384]{3,2,1,0:T(8,128)(2,1)} copy(bf16[1,32,64,384]{3,2,1,0:T(8,128)(2,1)S(1)} %bitcast.12) | data formatting | bytes 3145728
  77.1 1.3 %copy.15 = f32[8,256,64]{2,1,0:T(8,128)} copy(f32[8,256,64]{1,2,0:T(8,128)S(1)} %bitcast.13) | data formatting | bytes 1048576

commit v3 on v2

--- a/solution.py
+++ b/solution.py
@@ -20,7 +20,7 @@
     return lax.dot_general(lhs, rhs, (((1,), (0,)), ((), ())), preferred_element_type=F32)
 
 
-def layer_norm(src, dst, scale, shift):
+def layer_norm(src, dst, mid, scale, shift):
     dim, tm = src.shape
     chunks = [slice(i, i + 64) for i in range(0, dim, 64)]
 
@@ -29,19 +29,24 @@
         return jnp.sum(part, axis=0, keepdims=True) * (1.0 / dim)
 
     mean = total(src[rows, :] for rows in chunks)
-    var = total((src[rows, :] - mean) * (src[rows, :] - mean) for rows in chunks)
+    def squares():
+        for rows in chunks:
+            centered = src[rows, :] - mean
+            mid[rows, :] = centered
+            yield centered * centered
+    var = total(squares())
     inv = lax.rsqrt(var + 1e-6)
     for rows in chunks:
         for lane in range(0, tm, TILE):
             tile = slice(lane, lane + TILE)
-            dst[rows, tile] = ((src[rows, tile] - mean[:, tile]) * inv[:, tile] * scale[rows, :] + shift[rows, :]).astype(BF16)
+            dst[rows, tile] = (mid[rows, tile] * inv[:, tile] * scale[rows, :] + shift[rows, :]).astype(BF16)
 
 
 def kernel(dims, x_hbm, warm_hbm, wlat_hbm, wqkv_hbm, wo_hbm, wup_hbm, wdown_hbm, wout_hbm, mods_hbm, alpha_ref, beta_ref,
            xo_ref, hl_ref,
            wout_ref, mods_ref, wlat_raw, wqkv_raw, wo_raw, wup_raw, wdown_raw, warm_raw, x_raw,
            wlat_t, wqkv_t, wo_t, wup_t, wdown_t, modb,
-           h_ref, hb_ref, h2_ref, h2b_ref, u_ref, u2_ref, q_ref, k_ref, v_ref, att_ref, hid_ref,
+           mid_ref, mid2_ref, h_ref, hb_ref, h2_ref, h2b_ref, u_ref, u2_ref, q_ref, k_ref, v_ref, att_ref, hid_ref,
            b_in, x_in, b_out, x_out, x_f32,
            load_sem, hs_sem, hr_sem, xs_sem, xr_sem, fs_sem, fr_sem):
     steps, stages, heads, head_dim, dim, micro, tm = dims
@@ -75,44 +80,36 @@
                 modb[t, i, c * TILE:(c + 1) * TILE, :] = jnp.broadcast_to(row, (TILE, TILE)).T
 
     def make_inputs(m):
-        xt = x_raw[pl.ds(m * tm, tm), :].T
+        xt = x_raw[m * tm:(m + 1) * tm, :].T
         x_f32[m] = xt
         x_in[0, m] = xt.astype(BF16)
-
-        @pl.when(stage > 0)
-        def _():
-            b_in[0, m] = warm_raw[pl.ds(m * tm, tm), :].T
-
-        @pl.when(stage == 0)
-        def _():
-            for t in range(steps):
-                b_in[t, m] = jnp.zeros((dim, tm), BF16)
+        b_in[0, m] = warm_raw[m * tm:(m + 1) * tm, :].T
 
     mods.wait()
-
-    def mods_body(t, carry):
-        make_mods(t)
-        return carry
-    lax.fori_loop(0, steps, mods_body, 0)
+    make_mods(0)
     loads[0].wait()
     warm.wait()
 
-    def inputs_body(m, carry):
-        make_inputs(m)
-        return carry
-    lax.fori_loop(0, micro, inputs_body, 0)
-    for copy in loads[1:3]:
+    @pl.when(stage == 0)
+    def _():
+        warm_raw[...] = jnp.zeros_like(warm_raw)
+    for copy in loads[1:]:
         copy.wait()
+    make_inputs(0)
     wlat_t[...] = wlat_raw[...].T
     wqkv_t[...] = wqkv_raw[...].T
-    for copy in loads[3:]:
-        copy.wait()
 
     def late_weights():
         wo_t[...] = wo_raw[...].T
         for j in range(hidden // dim):
             wup_t[j * dim:(j + 1) * dim, :] = wup_raw[:, j * dim:(j + 1) * dim].T * jnp.asarray(0.5, BF16)
             wdown_t[:, j * dim:(j + 1) * dim] = wdown_raw[j * dim:(j + 1) * dim, :].T
+        for m in range(1, micro):
+            make_inputs(m)
+
+    def late_mods():
+        for t in range(1, steps):
+            make_mods(t)
 
     def h_copy(t, m):
         return pltpu.make_async_remote_copy(
@@ -142,11 +139,11 @@
     def attn_in(slot):
         t, m = step_of(slot)
         for rows in halves:
-            h_ref[rows, :] = b_in[t, m, rows, :].astype(F32) + dot(wlat_t[rows, :], x_in[t, m])
+            h_ref[rows, :] = b_in[jnp.where(stage > 0, t, 0), m, rows, :].astype(F32) + dot(wlat_t[rows, :], x_in[t, m])
 
     def attn_norm(slot):
         t, _ = step_of(slot)
-        layer_norm(h_ref, u_ref, modb.at[t, 1], modb.at[t, 0])
+        layer_norm(h_ref, u_ref, mid_ref, modb.at[t, 1], modb.at[t, 0])
 
     def project(part, dst):
         for rows in halves:
@@ -191,7 +188,7 @@
 
     def mlp_norm(slot):
         t, _ = step_of(slot)
-        layer_norm(h2_ref, u2_ref, modb.at[t, 4], modb.at[t, 3])
+        layer_norm(h2_ref, u2_ref, mid2_ref, modb.at[t, 4], modb.at[t, 3])
 
     def mlp_up(j):
         rows = slice(j * GROUP, (j + 1) * GROUP)
@@ -199,16 +196,12 @@
         inner = half * (half * half * (8.0 * GELU_A * GELU_B) + 2.0 * GELU_A)
         hid_ref[rows, :] = (half + half * jnp.tanh(inner)).astype(BF16)
 
-    def mlp_down(slot, part):
-        t, m = step_of(slot)
-        cut = slice(part * hidden // 2, (part + 1) * hidden // 2)
+    def mlp_down(slot):
+        t, m = step_of(slot)
         for rows in halves:
-            down = dot(wdown_t[rows, cut], hid_ref[cut, :])
+            down = dot(wdown_t[rows, :], hid_ref[...])
             for tile in tiles:
-                if part == 0:
-                    h2b_ref[rows, tile] = h2_ref[rows, tile] + modb[t, 5, rows, :] * down[:, tile]
-                else:
-                    b_out[t, m, rows, tile] = (h2b_ref[rows, tile] + modb[t, 5, rows, :] * down[:, tile]).astype(BF16)
+                b_out[t, m, rows, tile] = (h2b_ref[rows, tile] + modb[t, 5, rows, :] * down[:, tile]).astype(BF16)
 
     def latent(slot):
         t, m = step_of(slot)
@@ -248,11 +241,13 @@
         @pl.when(jnp.logical_and(t == steps - 1, stage == last))
         def _():
             xo_ref[m] = x_f32[m]
-            for dev in (5, 3, 1, 6):
+            for dev in (1, 3, 5, 6):
                 f_copy(m, x_f32, dev).start()
 
     def block(attn=None, out=None, mlp=None, lat=None, extra=None):
         ups = hidden // GROUP
+        if mlp is not None:
+            h2b_ref[...] = h2_ref[...]
         if out is not None:
             hb_ref[...] = h_ref[...]
         if attn is not None:
@@ -272,8 +267,6 @@
         if attn is not None:
             scores = score_dots()
             project(2, v_ref)
-        if mlp is not None:
-            mlp_down(mlp, 0)
         if out is not None:
             attn_out(out)
             mlp_norm(out)
@@ -282,13 +275,13 @@
         if attn is not None:
             value_dots([softmax(s) for s in scores])
         if mlp is not None:
-            mlp_down(mlp, 1)
+            mlp_down(mlp)
             send_stage(mlp)
         if lat is not None:
             send_latent(lat)
 
     block(attn=0, extra=late_weights)
-    block(attn=1, out=0)
+    block(attn=1, out=0, extra=late_mods)
     pl.semaphore_wait(barrier, stages - 1)
 
     def slot_body(slot, carry):
@@ -358,7 +351,7 @@
                 pltpu.VMEM((dim, ch), BF16), pltpu.VMEM((3 * dim, dim), BF16), pltpu.VMEM((dim, dim), BF16),
                 pltpu.VMEM((hidden, dim), BF16), pltpu.VMEM((dim, hidden), BF16),
                 pltpu.VMEM((steps, 6, dim, TILE), F32),
-                pltpu.VMEM((dim, tm), F32), pltpu.VMEM((dim, tm), F32), pltpu.VMEM((dim, tm), F32), pltpu.VMEM((dim, tm), F32),
+                pltpu.VMEM((dim, tm), F32), pltpu.VMEM((dim, tm), F32), pltpu.VMEM((dim, tm), F32), pltpu.VMEM((dim, tm), F32), pltpu.VMEM((dim, tm), F32), pltpu.VMEM((dim, tm), F32),
                 pltpu.VMEM((dim, tm), BF16), pltpu.VMEM((dim, tm), BF16),
                 pltpu.VMEM((dim, tm), BF16), pltpu.VMEM((dim, tm), BF16), pltpu.VMEM((dim, tm), BF16),
                 pltpu.VMEM((dim, tm), BF16), pltpu.VMEM((hidden, tm), BF16),

time: 78.5 us -> 76.9 us (0.980)
  Pallas kernels: 75.3 us -> 73.7 us
    pallas_call x1, Pallas kernels: 75.3 us -> 73.7 us  [stage_program(): pl.pallas_call(functools.partial(kernel, dims), out_shape=(pltpu.VMEM((mi...]
where the time goes in v3:
time: 76.9 us; the launch traced here: 76.8 us
  Pallas kernels  73.7 us (96%)
  local copies, waits for them, and re-layouts  2.45 us (3%)
    pallas_call x1, Pallas kernels, stage_program(): pl.pallas_call(functools.partial(kernel, dims), out_shape=(pltpu.VMEM((mi...  73.7 us
    unnamed x2, local copies, waits for them, and re-layouts  2.45 us

profile of v3, /device:TPU:0, one launch (start us, length us, event | category | flops | bytes accessed | tf_op | source)
XLA Modules:
  0.0 76.8 jit_solution(17474670544903312356)
XLA Ops:
  0.6 73.7 %shard_map.122 = (f32[8,64,256]{2,1,0:T(8,128)S(1)}, bf16[2048,384]{1,0:T(8,128)(2,1)S(1)}) custom-call(f32[2048,64]{1,0:T(8,128)} %bitcast.17, bf16[7,2048,384]{2,1,0:T(8,128)(2,1)} %bitcast.14, bf16[64,384]{1,0:T(8,128)(2,1)} %bitcast.21, bf16[384,1152]{1,0:T(8,128)(2,1)} %bitcast.19, bf16[384,384]{1,0:T(8,128)(2,1)} %bitcast.20, ...), custom_call_target="tpu_custom_call" | custom-call | tf_op jit(solution)/shard_map/pallas_call | solution.py:341
  74.3 1.1 %copy.18 = bf16[1,32,64,384]{3,2,1,0:T(8,128)(2,1)} copy(bf16[1,32,64,384]{3,2,1,0:T(8,128)(2,1)S(1)} %bitcast.12) | data formatting | bytes 3145728
  75.5 1.3 %copy.15 = f32[8,256,64]{2,1,0:T(8,128)} copy(f32[8,256,64]{1,2,0:T(8,128)S(1)} %bitcast.13) | data formatting | bytes 1048576

commit v4 on v3

--- a/solution.py
+++ b/solution.py
@@ -46,9 +46,9 @@
            xo_ref, hl_ref,
            wout_ref, mods_ref, wlat_raw, wqkv_raw, wo_raw, wup_raw, wdown_raw, warm_raw, x_raw,
            wlat_t, wqkv_t, wo_t, wup_t, wdown_t, modb,
-           mid_ref, mid2_ref, h_ref, hb_ref, h2_ref, h2b_ref, u_ref, u2_ref, q_ref, k_ref, v_ref, att_ref, hid_ref,
+           mid_ref, mid2_ref, h_ring, h2_ring, u_ref, u2_ref, q_ref, k_ref, v_ref, att_ref, hid_ref,
            b_in, x_in, b_out, x_out, x_f32,
-           load_sem, hs_sem, hr_sem, xs_sem, xr_sem, fs_sem, fr_sem):
+           load_sem, hs_sem, hr_sem, xs_sem, xr_sem, fs_sem, fr_sem, rs_sem):
     steps, stages, heads, head_dim, dim, micro, tm = dims
     stage = lax.axis_index('stage')
     last = stages - 1
@@ -123,7 +123,7 @@
 
     def f_copy(m, src, dev):
         return pltpu.make_async_remote_copy(
-            src_ref=src.at[m], dst_ref=xo_ref.at[m], send_sem=fs_sem.at[dev], recv_sem=fr_sem,
+            src_ref=src.at[m], dst_ref=xo_ref.at[m], send_sem=fs_sem.at[dev], recv_sem=fr_sem.at[lax.div(m, micro - 1)],
             device_id={'stage': dev}, device_id_type=MESH)
 
     low_half = lax.rem(lax.broadcasted_iota(jnp.int32, (head_dim, 2 * TILE), 1), TILE) < head_dim
@@ -139,11 +139,11 @@
     def attn_in(slot):
         t, m = step_of(slot)
         for rows in halves:
-            h_ref[rows, :] = b_in[jnp.where(stage > 0, t, 0), m, rows, :].astype(F32) + dot(wlat_t[rows, :], x_in[t, m])
+            h_ring[lax.rem(slot, 2), rows, :] = b_in[jnp.where(stage > 0, t, 0), m, rows, :].astype(F32) + dot(wlat_t[rows, :], x_in[t, m])
 
     def attn_norm(slot):
         t, _ = step_of(slot)
-        layer_norm(h_ref, u_ref, mid_ref, modb.at[t, 1], modb.at[t, 0])
+        layer_norm(h_ring.at[lax.rem(slot, 2)], u_ref, mid_ref, modb.at[t, 1], modb.at[t, 0])
 
     def project(part, dst):
         for rows in halves:
@@ -184,11 +184,11 @@
         for rows in halves:
             proj = dot(wo_t[rows, :], att_ref[...])
             for tile in tiles:
-                h2_ref[rows, tile] = hb_ref[rows, tile] + modb[t, 2, rows, :] * proj[:, tile]
+                h2_ring[lax.rem(slot, 2), rows, tile] = h_ring[lax.rem(slot, 2), rows, tile] + modb[t, 2, rows, :] * proj[:, tile]
 
     def mlp_norm(slot):
         t, _ = step_of(slot)
-        layer_norm(h2_ref, u2_ref, mid2_ref, modb.at[t, 4], modb.at[t, 3])
+        layer_norm(h2_ring.at[lax.rem(slot, 2)], u2_ref, mid2_ref, modb.at[t, 4], modb.at[t, 3])
 
     def mlp_up(j):
         rows = slice(j * GROUP, (j + 1) * GROUP)
@@ -201,7 +201,7 @@
         for rows in halves:
             down = dot(wdown_t[rows, :], hid_ref[...])
             for tile in tiles:
-                b_out[t, m, rows, tile] = (h2b_ref[rows, tile] + modb[t, 5, rows, :] * down[:, tile]).astype(BF16)
+                b_out[t, m, rows, tile] = (h2_ring[lax.rem(slot, 2), rows, tile] + modb[t, 5, rows, :] * down[:, tile]).astype(BF16)
 
     def latent(slot):
         t, m = step_of(slot)
@@ -241,15 +241,14 @@
         @pl.when(jnp.logical_and(t == steps - 1, stage == last))
         def _():
             xo_ref[m] = x_f32[m]
+            @pl.when(m == micro - 1)
+            def _():
+                f_copy(m, x_f32, 0).start()
             for dev in (1, 3, 5, 6):
                 f_copy(m, x_f32, dev).start()
 
     def block(attn=None, out=None, mlp=None, lat=None, extra=None):
         ups = hidden // GROUP
-        if mlp is not None:
-            h2b_ref[...] = h2_ref[...]
-        if out is not None:
-            hb_ref[...] = h_ref[...]
         if attn is not None:
             attn_in(attn)
         if lat is not None:
@@ -297,32 +296,42 @@
 
     def whole(src, dst, sem, dev):
         return pltpu.make_async_remote_copy(
-            src_ref=src, dst_ref=dst, send_sem=sem, recv_sem=fr_sem, device_id={'stage': dev}, device_id_type=MESH)
+            src_ref=src, dst_ref=dst, send_sem=sem, recv_sem=fr_sem.at[0], device_id={'stage': dev}, device_id_type=MESH)
+
+    def relay(part, dev):
+        span = pl.ds(0, micro - 1) if part == 0 else pl.ds(micro - 1, 1)
+        return pltpu.make_async_remote_copy(
+            src_ref=xo_ref.at[span], dst_ref=xo_ref.at[span], send_sem=rs_sem.at[part], recv_sem=fr_sem.at[part],
+            device_id={'stage': dev}, device_id_type=MESH)
 
     sent = pl.ds(0, steps - 1)
-
-    @pl.when(stage < last)
-    def _():
-        whole(xo_ref, xo_ref, fs_sem.at[0], 0).wait_recv()
-    for src, dev in ((5, 4), (3, 2), (1, 0)):
-        @pl.when(stage == src)
-        def _(dev=dev):
-            whole(xo_ref, xo_ref, fs_sem.at[dev], dev).start()
+    for part in range(2):
+        @pl.when(stage < last)
+        def _(part=part):
+            relay(part, 0).wait_recv()
+        for src, dev in ((5, 4), (3, 2), (1, 0)):
+            if part == 0 or dev > 0:
+                @pl.when(stage == src)
+                def _(part=part, dev=dev):
+                    relay(part, dev).start()
 
     @pl.when(stage < last)
     def _():
         whole(b_out.at[sent], b_in.at[pl.ds(1, steps - 1)], hs_sem, jnp.minimum(stage + 1, last)).wait_send()
     for src, dev in ((5, 4), (3, 2), (1, 0)):
-        @pl.when(stage == src)
-        def _(dev=dev):
-            whole(xo_ref, xo_ref, fs_sem.at[dev], dev).wait_send()
+        for part in range(2):
+            if part == 0 or dev > 0:
+                @pl.when(stage == src)
+                def _(part=part, dev=dev):
+                    relay(part, dev).wait_send()
 
     @pl.when(stage == last)
     def _():
         for dev in others:
             whole(x_out.at[sent], x_in.at[pl.ds(1, steps - 1)], xs_sem.at[dev], dev).wait_send()
-        for dev in (5, 3, 1, 6):
+        for dev in (1, 3, 5, 6):
             whole(x_f32, xo_ref, fs_sem.at[dev], dev).wait_send()
+        f_copy(micro - 1, x_f32, 0).wait_send()
 
 
 def solution(mesh):
@@ -351,7 +360,7 @@
                 pltpu.VMEM((dim, ch), BF16), pltpu.VMEM((3 * dim, dim), BF16), pltpu.VMEM((dim, dim), BF16),
                 pltpu.VMEM((hidden, dim), BF16), pltpu.VMEM((dim, hidden), BF16),
                 pltpu.VMEM((steps, 6, dim, TILE), F32),
-                pltpu.VMEM((dim, tm), F32), pltpu.VMEM((dim, tm), F32), pltpu.VMEM((dim, tm), F32), pltpu.VMEM((dim, tm), F32), pltpu.VMEM((dim, tm), F32), pltpu.VMEM((dim, tm), F32),
+                pltpu.VMEM((dim, tm), F32), pltpu.VMEM((dim, tm), F32), pltpu.VMEM((2, dim, tm), F32), pltpu.VMEM((2, dim, tm), F32),
                 pltpu.VMEM((dim, tm), BF16), pltpu.VMEM((dim, tm), BF16),
                 pltpu.VMEM((dim, tm), BF16), pltpu.VMEM((dim, tm), BF16), pltpu.VMEM((dim, tm), BF16),
                 pltpu.VMEM((dim, tm), BF16), pltpu.VMEM((hidden, tm), BF16),
@@ -360,7 +369,7 @@
                 pltpu.SemaphoreType.DMA((9,)),
                 pltpu.SemaphoreType.DMA, pltpu.SemaphoreType.DMA((steps - 1, micro)),
                 pltpu.SemaphoreType.DMA((stages,)), pltpu.SemaphoreType.DMA((steps - 1, micro)),
-                pltpu.SemaphoreType.DMA((stages,)), pltpu.SemaphoreType.DMA,
+                pltpu.SemaphoreType.DMA((stages,)), pltpu.SemaphoreType.DMA((2,)), pltpu.SemaphoreType.DMA((2,)),
             ],
             compiler_params=pltpu.CompilerParams(collective_id=0, has_side_effects=True, vmem_limit_bytes=60 * 1024 * 1024),
         )(x_init.reshape(total, ch), h_warm.reshape(stages - 1, total, dim), w_lat.reshape(ch, dim),

time: 76.9 us -> 75.8 us (0.986)
  Pallas kernels: 73.7 us -> 72.6 us
    pallas_call x1, Pallas kernels: 73.7 us -> 72.6 us  [stage_program(): pl.pallas_call(functools.partial(kernel, dims), out_shape=(pltpu.VMEM((mi...]
where the time goes in v4:
time: 75.8 us; the launch traced here: 75.7 us
  Pallas kernels  72.6 us (96%)
  local copies, waits for them, and re-layouts  2.45 us (3%)
    pallas_call x1, Pallas kernels, stage_program(): pl.pallas_call(functools.partial(kernel, dims), out_shape=(pltpu.VMEM((mi...  72.6 us
    unnamed x2, local copies, waits for them, and re-layouts  2.45 us

profile of v4, /device:TPU:0, one launch (start us, length us, event | category | flops | bytes accessed | tf_op | source)
XLA Modules:
  0.0 75.7 jit_solution(7789391314548489267)
XLA Ops:
  0.6 72.6 %shard_map.122 = (f32[8,64,256]{2,1,0:T(8,128)S(1)}, bf16[2048,384]{1,0:T(8,128)(2,1)S(1)}) custom-call(f32[2048,64]{1,0:T(8,128)} %bitcast.17, bf16[7,2048,384]{2,1,0:T(8,128)(2,1)} %bitcast.14, bf16[64,384]{1,0:T(8,128)(2,1)} %bitcast.21, bf16[384,1152]{1,0:T(8,128)(2,1)} %bitcast.19, bf16[384,384]{1,0:T(8,128)(2,1)} %bitcast.20, ...), custom_call_target="tpu_custom_call" | custom-call | tf_op jit(solution)/shard_map/pallas_call | solution.py:350
  73.2 1.1 %copy.18 = bf16[1,32,64,384]{3,2,1,0:T(8,128)(2,1)} copy(bf16[1,32,64,384]{3,2,1,0:T(8,128)(2,1)S(1)} %bitcast.12) | data formatting | bytes 3145728
  74.4 1.3 %copy.15 = f32[8,256,64]{2,1,0:T(8,128)} copy(f32[8,256,64]{1,2,0:T(8,128)S(1)} %bitcast.13) | data formatting | bytes 1048576

commit v5 on v4

--- a/solution.py
+++ b/solution.py
@@ -93,11 +93,13 @@
     @pl.when(stage == 0)
     def _():
         warm_raw[...] = jnp.zeros_like(warm_raw)
-    for copy in loads[1:]:
+    for copy in loads[1:3]:
         copy.wait()
     make_inputs(0)
     wlat_t[...] = wlat_raw[...].T
     wqkv_t[...] = wqkv_raw[...].T
+    for copy in loads[3:]:
+        copy.wait()
 
     def late_weights():
         wo_t[...] = wo_raw[...].T

time: 75.8 us -> 75.5 us (level)
  no operation moved by 1% of the time
where the time goes in v5:
time: 75.5 us; the launch traced here: 75.4 us
  Pallas kernels  72.3 us (96%)
  local copies, waits for them, and re-layouts  2.45 us (3%)
    pallas_call x1, Pallas kernels, stage_program(): pl.pallas_call(functools.partial(kernel, dims), out_shape=(pltpu.VMEM((mi...  72.3 us
    unnamed x2, local copies, waits for them, and re-layouts  2.45 us

profile of v5, /device:TPU:0, one launch (start us, length us, event | category | flops | bytes accessed | tf_op | source)
XLA Modules:
  0.0 75.4 jit_solution(18269298251373505507)
XLA Ops:
  0.6 72.3 %shard_map.122 = (f32[8,64,256]{2,1,0:T(8,128)S(1)}, bf16[2048,384]{1,0:T(8,128)(2,1)S(1)}) custom-call(f32[2048,64]{1,0:T(8,128)} %bitcast.17, bf16[7,2048,384]{2,1,0:T(8,128)(2,1)} %bitcast.14, bf16[64,384]{1,0:T(8,128)(2,1)} %bitcast.21, bf16[384,1152]{1,0:T(8,128)(2,1)} %bitcast.19, bf16[384,384]{1,0:T(8,128)(2,1)} %bitcast.20, ...), custom_call_target="tpu_custom_call" | custom-call | tf_op jit(solution)/shard_map/pallas_call | solution.py:352
  73.0 1.1 %copy.18 = bf16[1,32,64,384]{3,2,1,0:T(8,128)(2,1)} copy(bf16[1,32,64,384]{3,2,1,0:T(8,128)(2,1)S(1)} %bitcast.12) | data formatting | bytes 3145728
  74.1 1.3 %copy.15 = f32[8,256,64]{2,1,0:T(8,128)} copy(f32[8,256,64]{1,2,0:T(8,128)S(1)} %bitcast.13) | data formatting | bytes 1048576
